TPU v7x, 32 devices: a whole 2x2x4 slice. The times are simulated.
32 devices in a mesh: ctx: 8 (over y, x, core), fsdp: 4 (over z).
Axes of the slice: x: 2, y: 2, z: 4, core: 2. Of those that a mesh axis runs over, the one named last changes fastest.
Arguments:
- inputs: bfloat16 [4, 1024, 1536], P('fsdp', 'ctx')
- positions: int32 [4, 1024], P('fsdp', 'ctx'), may hold values from 0 to 1535, as said below
- block_order: int32 [16], replicated, may hold values from 0 to 15, as said below
- attention_gain: bfloat16 [1536], P('fsdp'), may hold values from 0.5 to 1.5
- projection: bfloat16 [1536, 2048], P('fsdp')
- projection_bias: bfloat16 [2048], P('fsdp'), may hold values from -4 to 4
- output_weight: bfloat16 [1536, 1536], P('fsdp'), may hold values from -1.5 to 1.5
- feedforward_gain: bfloat16 [1536], P('fsdp'), may hold values from 0.5 to 1.5
- gate_up: bfloat16 [1536, 17920], P('fsdp'), may hold values from -0.15625 to 0.15625
- down_weight: bfloat16 [8960, 1536], P('fsdp'), may hold values from -0.0625 to 0.0625
- cotangent: bfloat16 [4, 1024, 1536], P('fsdp', 'ctx'), may hold values from -6 to 6
Outputs:
- outputs: bfloat16 [4, 1024, 1536], P('fsdp', 'ctx')
- gradient: bfloat16 [4, 1024, 1536], P('fsdp', 'ctx')
- gradient_attention_gain: float32 [1536], P(('ctx', 'fsdp'))
- gradient_projection: float32 [1536, 2048], P('fsdp', 'ctx')
- gradient_projection_bias: float32 [2048], P(('ctx', 'fsdp'))
- gradient_output: float32 [1536, 1536], P('fsdp', 'ctx')
- gradient_feedforward_gain: float32 [1536], P(('ctx', 'fsdp'))
- gradient_gate_up: float32 [1536, 17920], P('fsdp', 'ctx')
- gradient_down: float32 [8960, 1536], P('fsdp', 'ctx')
Inputs may be any that keep to these rules, and one draw needn't show every extreme that they name: `block_order`: A permutation: each of 0 to 15 appears once. Within each sequence, positions grow strictly with order_index; the sequence's first token has position 0, and of the 1023 steps between tokens next to each other in the sequence exactly 512 are 2 and the others are 1, so the last token has position 1535.
All inputs are finite; a program needn't handle non-finite values.
Results may differ from a plain program's by a relative error of at most 0.02.
Values may be sent and summed in bfloat16 or wider, within the bound.
A program may use at most 320 MiB of HBM per device.

v0:
```python
import math
import jax
import jax.numpy as jnp
from jax import lax
from jax.sharding import PartitionSpec as P

HEADS = 12
KV_HEADS = 2
HEAD = 128
FF = 8960
GROUP = 2
EPS = 1e-06
THETA = 1000000.0
NEGATIVE = -1e30
BF = jnp.bfloat16
F32 = jnp.float32


def rope_tables(places):
    freq = THETA ** (-jnp.arange(0, HEAD, 2).astype(F32) / HEAD)
    angle = places.astype(F32)[:, None] * freq[None, :]
    angle = jnp.concatenate([angle, angle], axis=-1)
    return (jnp.cos(angle), jnp.sin(angle))


def rotate(values):
    middle = values.shape[-1] // 2
    return jnp.concatenate([-values[..., middle:], values[..., :middle]], axis=-1)


def apply_rope(values, cosine, sine):
    return values * cosine[:, None, :] + rotate(values) * sine[:, None, :]


def rope_back(grads, cosine, sine):
    return grads * cosine[:, None, :] - rotate(grads * sine[:, None, :])


def order_rows(block_order, start, count, half):
    offsets = start + jnp.arange(count, dtype=jnp.int32)
    slots = offsets // half
    table = jnp.arange(block_order.shape[0], dtype=jnp.int32)
    picked = jnp.sum(jnp.where(slots[:, None] == table[None, :], block_order[None, :], 0), axis=1)
    return picked * half + offsets % half


def rms_inverse(values):
    return lax.rsqrt(jnp.mean(values * values, axis=-1, keepdims=True) + EPS)


def norm_back(d_normed, values, inverse, gain):
    unit = values * inverse
    d_unit = d_normed * gain
    d_gain = jnp.sum(d_normed * unit, axis=0)
    d_values = inverse * (d_unit - unit * jnp.mean(d_unit * unit, axis=-1, keepdims=True))
    return (d_values, d_gain)


def dot(left, right, dims, out=F32):
    return lax.dot_general(left, right, (dims, ((), ())), preferred_element_type=out)


def swapped(x, size):
    return lax.ppermute(x, "fsdp", [(i, i ^ 1) for i in range(size)])


def gather_tokens(x, size):
    both = jnp.stack([x, swapped(x, size)])
    return lax.all_gather(both, "ctx", axis=1, tiled=True)


def scatter_tokens(partial, size):
    parts = lax.psum_scatter(partial, "ctx", scatter_dimension=1, tiled=True)
    return parts[0].astype(F32) + swapped(parts[1], size).astype(F32)


def body(
    inputs,
    positions,
    block_order,
    attention_gain,
    projection,
    projection_bias,
    output_weight,
    feedforward_gain,
    gate_up,
    down_weight,
    cotangent,
):
    rows, width = inputs.shape[1:]
    half = rows // 2
    ratio = HEADS // KV_HEADS
    query_width = HEADS * HEAD
    key_width = KV_HEADS * HEAD
    cycle = lax.axis_size("ctx")
    owners = lax.axis_size("fsdp")
    place = lax.axis_index("ctx")
    owner = lax.axis_index("fsdp")
    fold = owners // GROUP
    unit = FF // (owners * cycle)
    depth = width // owners
    length = rows * cycle
    slab = depth // cycle
    whole_projection = lax.all_gather(
        lax.dynamic_slice_in_dim(projection, place * slab, slab, 0),
        ("fsdp", "ctx"),
        axis=0,
        tiled=True,
    )
    whole_output = lax.all_gather(
        lax.dynamic_slice_in_dim(output_weight, place * slab, slab, 0),
        ("fsdp", "ctx"),
        axis=0,
        tiled=True,
    )
    small = lax.all_gather(
        jnp.concatenate([attention_gain, feedforward_gain, projection_bias]), "fsdp", axis=0
    )
    gain_one = small[:, :depth].reshape(-1).astype(F32)
    gain_two = small[:, depth : 2 * depth].reshape(-1).astype(F32)
    bias = small[:, 2 * depth :].reshape(-1).astype(F32)
    pieces = []
    for side in range(2):
        for plane in range(owners):
            start = side * FF + plane * (FF // owners) + place * unit
            pieces.append(lax.dynamic_slice_in_dim(gate_up, start, unit, 1))

    def part(side, to):
        return jnp.concatenate(
            [pieces[side * owners + (to + GROUP * b) % owners] for b in range(fold)], axis=1
        )

    sent = jnp.stack([jnp.stack([part(side, to) for side in range(2)]) for to in range(owners)])
    got = lax.all_to_all(sent, "fsdp", split_axis=0, concat_axis=0, tiled=True)
    gate_weight = got[:, 0].reshape(width, fold * unit)
    up_weight = got[:, 1].reshape(width, fold * unit)
    own_down = lax.dynamic_slice_in_dim(down_weight, place * unit, unit, 0)
    down = [own_down]
    for b in range(1, fold):
        route = [((i + GROUP * b) % owners, i) for i in range(owners)]
        down.append(lax.ppermute(own_down, "fsdp", route))
    down = jnp.concatenate(down, axis=0)
    tangent = cotangent[0]
    tangents = gather_tokens(tangent, owners).reshape(GROUP * length, width)
    features = inputs[0].astype(F32)
    inverse_one = rms_inverse(features)
    normed_one = (features * inverse_one * gain_one).astype(BF)
    projected = dot(normed_one, whole_projection, ((1,), (0,))) + bias
    cosine, sine = rope_tables(positions[0])
    queries = apply_rope(
        projected[:, :query_width].reshape(rows, HEADS, HEAD), cosine, sine
    ).astype(BF)
    keys = apply_rope(
        projected[:, query_width : query_width + key_width].reshape(rows, KV_HEADS, HEAD),
        cosine,
        sine,
    ).astype(BF)
    values = projected[:, query_width + key_width :].astype(BF)
    pairs = lax.all_gather(
        jnp.concatenate([keys.reshape(rows, key_width), values], axis=1), "ctx", axis=0, tiled=True
    )
    all_keys = pairs[:, :key_width].reshape(length, KV_HEADS, HEAD)
    all_values = pairs[:, key_width:].reshape(length, KV_HEADS, HEAD)
    grouped = queries.reshape(rows, KV_HEADS, ratio, HEAD).transpose(1, 2, 0, 3)
    own_index = order_rows(block_order, place * rows, rows, half)
    all_index = order_rows(block_order, 0, length, half)
    mask = (all_index[None, :] <= own_index[:, None])[None, None]
    scale = 1.0 / math.sqrt(HEAD)

    def weights_of():
        scores = jnp.einsum("grqd,kgd->grqk", grouped, all_keys, preferred_element_type=F32) * scale
        return jnp.where(mask, scores, NEGATIVE)

    scores = weights_of()
    top = jnp.max(scores, axis=-1, keepdims=True)
    probs = jnp.exp(scores - top)
    total = jnp.sum(probs, axis=-1, keepdims=True)
    probs = probs / total
    low_probs = probs.astype(BF)
    attention = jnp.einsum("grqk,kgd->grqd", low_probs, all_values, preferred_element_type=F32)
    merged = attention.transpose(2, 0, 1, 3).reshape(rows, query_width).astype(BF)
    residual = features + dot(merged, whole_output, ((1,), (0,)))
    inverse_two = rms_inverse(residual)
    normed_two = (residual * inverse_two * gain_two).astype(BF)
    tokens = gather_tokens(normed_two, owners).reshape(GROUP * length, width)
    gate = dot(tokens, gate_weight, ((1,), (0,)))
    upward = dot(tokens, up_weight, ((1,), (0,)))
    sigmoid = jax.nn.sigmoid(gate)
    activation = (gate * sigmoid * upward).astype(BF)
    branch = dot(activation, down, ((1,), (0,)), BF).reshape(GROUP, length, width)
    outputs = (residual + scatter_tokens(branch, owners)).astype(BF)
    d_activation = dot(tangents, down, ((1,), (1,)))
    d_gate = (d_activation * upward * sigmoid * (1.0 + gate * (1.0 - sigmoid))).astype(BF)
    d_upward = (d_activation * gate * sigmoid).astype(BF)
    d_tokens = (
        dot(d_gate, gate_weight, ((1,), (1,))) + dot(d_upward, up_weight, ((1,), (1,)))
    ).astype(BF)
    d_normed_two = scatter_tokens(d_tokens.reshape(GROUP, length, width), owners)
    grad_gate = dot(tokens, d_gate, ((0,), (0,)), BF)
    grad_up = dot(tokens, d_upward, ((0,), (0,)), BF)
    grad_down = dot(activation, tangents, ((0,), (0,)), BF)
    mine = lax.all_to_all(
        jnp.stack([grad_gate.reshape(owners, depth, -1), grad_up.reshape(owners, depth, -1)], 1),
        "fsdp",
        split_axis=0,
        concat_axis=0,
        tiled=True,
    )
    folded = []
    for plane in range(owners):
        total_piece = 0.0
        for source in range(plane % GROUP, owners, GROUP):
            b = (plane - source) // GROUP % fold
            total_piece = total_piece + mine[source, :, :, b * unit : (b + 1) * unit].astype(F32)
        folded.append(total_piece.astype(BF))
    folded = jnp.stack(folded, axis=1)
    spread = lax.all_to_all(
        folded.reshape(cycle, 2 * owners // cycle, depth, unit),
        "ctx",
        split_axis=0,
        concat_axis=0,
        tiled=True,
    )
    final_gate_up = spread.transpose(2, 1, 0, 3).reshape(depth, -1).astype(F32)
    grad_down = grad_down.reshape(fold, unit, width)
    total_down = grad_down[0].astype(F32)
    for b in range(1, fold):
        route = [(i, (i + GROUP * b) % owners) for i in range(owners)]
        total_down = total_down + lax.ppermute(grad_down[b], "fsdp", route).astype(F32)
    final_down = (
        lax.all_to_all(
            total_down.astype(BF).reshape(unit, cycle, width // cycle).transpose(1, 0, 2),
            "ctx",
            split_axis=0,
            concat_axis=0,
            tiled=True,
        )
        .reshape(-1, width // cycle)
        .astype(F32)
    )
    d_residual, grad_gain_two = norm_back(d_normed_two, residual, inverse_two, gain_two)
    d_residual = d_residual + tangent.astype(F32)
    d_branch = d_residual.astype(BF)
    d_merged = dot(d_branch, whole_output, ((1,), (1,))).astype(BF)
    d_attention = d_merged.reshape(rows, KV_HEADS, ratio, HEAD).transpose(1, 2, 0, 3)
    delta = jnp.sum(d_attention.astype(F32) * attention, axis=-1, keepdims=True)
    d_values = jnp.einsum("grqk,grqd->kgd", low_probs, d_attention, preferred_element_type=F32)
    d_probs = jnp.einsum("grqd,kgd->grqk", d_attention, all_values, preferred_element_type=F32)
    d_scores = (probs * (d_probs - delta)).astype(BF)
    d_queries = jnp.einsum("grqk,kgd->qgrd", d_scores, all_keys, preferred_element_type=F32) * scale
    d_keys = jnp.einsum("grqk,grqd->kgd", d_scores, grouped, preferred_element_type=F32) * scale
    d_pairs = jnp.concatenate(
        [d_keys.reshape(length, key_width), d_values.reshape(length, key_width)], axis=1
    ).astype(BF)
    d_pairs = lax.psum_scatter(d_pairs, "ctx", scatter_dimension=0, tiled=True).astype(F32)
    d_query_raw = rope_back(d_queries.reshape(rows, HEADS, HEAD), cosine, sine)
    d_key_raw = rope_back(d_pairs[:, :key_width].reshape(rows, KV_HEADS, HEAD), cosine, sine)
    d_projected = jnp.concatenate(
        [
            d_query_raw.reshape(rows, query_width),
            d_key_raw.reshape(rows, key_width),
            d_pairs[:, key_width:],
        ],
        axis=1,
    ).astype(BF)
    grad_bias = jnp.sum(d_projected.astype(F32), axis=0)
    d_normed_one = dot(d_projected, whole_projection, ((1,), (1,)))
    d_features, grad_gain_one = norm_back(d_normed_one, features, inverse_one, gain_one)
    gradient = (d_residual + d_features).astype(BF)

    def columns_home(left, right):
        whole_left = lax.all_gather(left, "ctx", axis=0, tiled=True)
        share = right.shape[1] // cycle
        sliced = lax.all_to_all(
            right.reshape(rows, cycle, share).transpose(1, 0, 2),
            "ctx",
            split_axis=0,
            concat_axis=0,
            tiled=True,
        ).reshape(length, share)
        partial = dot(whole_left, sliced, ((0,), (0,)), BF).reshape(owners, depth, share)
        parts = lax.all_to_all(partial, "fsdp", split_axis=0, concat_axis=0, tiled=True)
        return jnp.sum(parts.astype(F32), axis=0)

    final_output = columns_home(merged, d_branch)
    final_projection = columns_home(normed_one, d_projected)
    count = owners * cycle
    sums = jnp.concatenate(
        [
            grad_gain_one.reshape(count, -1),
            grad_bias.reshape(count, -1),
            grad_gain_two.reshape(count, -1),
        ],
        axis=1,
    )
    sums = lax.psum_scatter(sums, ("ctx", "fsdp"), scatter_dimension=0, tiled=True)[0]
    first = width // count
    last = sums.shape[0] - first
    return (
        outputs[None],
        gradient[None],
        sums[:first],
        final_projection,
        sums[first:last],
        final_output,
        sums[last:],
        final_gate_up,
        final_down,
    )


def solution(mesh):
    return jax.shard_map(
        body,
        mesh=mesh,
        in_specs=(
            P("fsdp", "ctx", None),
            P("fsdp", "ctx"),
            P(),
            P("fsdp"),
            P("fsdp", None),
            P("fsdp"),
            P("fsdp", None),
            P("fsdp"),
            P("fsdp", None),
            P("fsdp", None),
            P("fsdp", "ctx", None),
        ),
        out_specs=(
            P("fsdp", "ctx", None),
            P("fsdp", "ctx", None),
            P(("ctx", "fsdp")),
            P("fsdp", "ctx"),
            P(("ctx", "fsdp")),
            P("fsdp", "ctx"),
            P(("ctx", "fsdp")),
            P("fsdp", "ctx"),
            P("fsdp", "ctx"),
        ),
        check_vma=False,
    )
```

profile of v0, /device:TPU:0, one launch (start us, length us, event | category | flops | bytes accessed | tf_op | source)
XLA Modules:
  0.0 765.0 jit_solution(17226624631359661983)
XLA Ops:
  10.1 14.9 %all-gather.1 = bf16[4,1,1280]{2,1,0:T(2,128)(2,1)S(1)} all-gather(bf16[1,1,1280]{2,1,0:T(2,128)(2,1)S(1)} %reshape.500), channel_id=2, replica_groups=mesh['ctx'=8,'fsdp'=4] {'fsdp'}, dimensions={0}, use_global_device_ids=true | all-gather | bytes 12800 | tf_op jit(solution)/shard_map/all_gather | solution.py:116
  28.6 54.7 %all-gather.10.cloned.1.call-done = bf16[1536,2048]{1,0:T(8,128)(2,1)} async-done(((bf16[48,2048]{1,0:T(8,128)(2,1)}), bf16[1536,2048]{1,0:T(8,128)(2,1)}) %all-gather.10.cloned.1.call-update) | async-done | bytes 6291472 | tf_op jit(solution)/shard_map/all_gather | solution.py:104
  83.3 3.8 convolution_add_fusion.1
  91.2 19.4 %all-gather.12.cloned.1.call-done = bf16[1024,512]{1,0:T(8,128)(2,1)} async-done(((bf16[128,512]{1,0:T(8,128)(2,1)}), bf16[1024,512]{1,0:T(8,128)(2,1)}) %all-gather.12.cloned.1.call-update) | async-done | bytes 1048592 | tf_op jit(solution)/shard_map/all_gather | solution.py:159
  112.5 4.8 fusion.70
  117.4 3.5 fusion.5
  123.7 53.9 %all-gather.14.cloned.1.call-done = bf16[1536,1536]{1,0:T(8,128)(2,1)} async-done(((bf16[48,1536]{1,0:T(8,128)(2,1)}), bf16[1536,1536]{1,0:T(8,128)(2,1)}) %all-gather.14.cloned.1.call-update) | async-done | bytes 4718608 | tf_op jit(solution)/shard_map/all_gather | solution.py:110
  177.7 3.2 multiply_reduce_fusion.3
  182.7 9.7 %collective-permute-done = bf16[128,1536]{1,0:T(8,128)(2,1)S(1)} collective-permute-done((bf16[128,1536]{1,0:T(8,128)(2,1)S(1)}, bf16[128,1536]{1,0:T(8,128)(2,1)S(1)}, u32[]{:S(2)}, u32[]{:S(2)}) %collective-permute-start) | collective-permute-done | bytes 393248 | tf_op jit(solution)/shard_map/ppermute | solution.py:64
  195.1 9.0 %collective-permute-done.3 = bf16[128,1536]{1,0:T(8,128)(2,1)S(1)} collective-permute-done((bf16[128,1536]{1,0:T(8,128)(2,1)S(1)}, bf16[128,1536]{1,0:T(8,128)(2,1)S(1)}, u32[]{:S(2)}, u32[]{:S(2)}) %collective-permute-start.3) | collective-permute-done | bytes 393248 | tf_op jit(solution)/shard_map/ppermute | solution.py:64
  205.1 4.2 constant_dynamic-slice_fusion.5
  209.3 1.8 copy.197
  211.1 1.8 copy.198
  212.9 1.8 copy.199
  214.7 1.8 copy.200
  222.6 2.0 pad_maximum_fusion
  224.6 4.7 all-to-all-start
  230.6 2.9 collective-permute-start.1
  233.5 91.3 %all-to-all-done = bf16[4,2,384,560]{2,3,1,0:T(8,128)(2,1)} async-done(((bf16[4,2,384,560]{2,3,1,0:T(8,128)(2,1)}), bf16[4,2,384,560]{2,3,1,0:T(8,128)(2,1)}, u32[]{:S(2)}, u32[]{:S(2)}) %all-to-all-start) | async-done | bytes 3440672 | tf_op jit(solution)/shard_map/all_to_all | solution.py:134
  324.8 2.3 fusion.68
  331.4 9.2 %fusion.73 = f32[2048,560]{0,1:T(8,128)} fusion(bf16[2048,1536]{1,0:T(8,128)(2,1)} %bitcast.252, bf16[1536,560]{0,1:T(8,128)(2,1)} %bitcast.274), kind=kOutput, calls=%fused_computation.187 | convolution fusion | flops 3523215360 | bytes 12599296 | tf_op jit(solution)/shard_map/dot_general | solution.py:60
  340.6 5.8 fusion.72
  346.4 10.8 %multiply_convert_fusion.1 = (bf16[2048,560]{0,1:T(8,128)(2,1)S(1)}, bf16[2048,560]{0,1:T(8,128)(2,1)S(1)}, bf16[2048,560]{0,1:T(8,128)(2,1)}) fusion(f32[2048,560]{0,1:T(8,128)} %fusion.72, f32[2048,560]{0,1:T(8,128)} %fusion.73, bf16[2048,1536]{1,0:T(8,128)(2,1)} %bitcast.290, bf16[280,1536]{1,0:T(8,128)(2,1)} %collective-permute-done.1, ...), kind=kOutput, calls=%fused_computation.6 | convolution fusion | flops 3545006080 | bytes 24068096 | tf_op jit(solution)/shard_map/dot_general | solution.py:60
  357.2 5.1 fusion.74
  362.4 7.0 add_convert_fusion
  371.0 8.9 %copy.168 = bf16[1536,2048]{1,0:T(8,128)(2,1)} copy(bf16[1536,2048]{0,1:T(8,128)(2,1)} %bitcast.253) | data formatting | bytes 12582912 | tf_op jit(solution)/shard_map/dot_general | solution.py:60
  379.9 50.9 %reduce-scatter.6.cloned.1.call-done = bf16[2,128,1536]{2,1,0:T(8,128)(2,1)} async-done(((bf16[2,1024,1536]{2,1,0:T(8,128)(2,1)}), bf16[2,128,1536]{2,1,0:T(8,128)(2,1)}) %reduce-scatter.6.cloned.1.call-update) | async-done | bytes 786448 | tf_op jit(solution)/shard_map/reduce_scatter | solution.py:73
  433.4 8.5 %fusion.10 = bf16[4,1,384,560]{2,3,0,1:T(8,128)(2,1)} fusion(bf16[4,384,2048]{2,1,0:T(8,128)(2,1)} %bitcast.256, bf16[2048,560]{0,1:T(8,128)(2,1)} %copy-done.46), kind=kOutput, calls=%fused_computation.28 | convolution fusion | flops 3523215360 | bytes 10305536 | tf_op jit(solution)/shard_map/dot_general | solution.py:60
  443.3 4.7 convolution_convert_fusion
  449.3 3.9 multiply_convert_fusion
  453.2 1.6 copy-done.3
  455.7 3.3 fusion.18
  461.3 7.5 fusion.13
  469.2 2.1 copy.169
  471.3 4.9 all-to-all-start.5
  476.3 9.2 %fusion.24 = bf16[2048,1536]{1,0:T(8,128)(2,1)} fusion(bf16[2048,560]{0,1:T(8,128)(2,1)} %get-tuple-element.25, bf16[280,1536]{1,0:T(8,128)(2,1)} %collective-permute-done.1, bf16[280,1536]{1,0:T(8,128)(2,1)S(1)} %copy-done.31), kind=kOutput, calls=%fused_computation.46 | convolution fusion | flops 3526656000 | bytes 10305536 | tf_op jit(solution)/shard_map/dot_general | solution.py:60
  485.5 7.7 %fusion.77 = bf16[560,1536]{1,0:T(8,128)(2,1)S(1)} fusion(bf16[2048,560]{0,1:T(8,128)(2,1)} %get-tuple-element.25, bf16[2048,1536]{1,0:T(8,128)(2,1)} %bitcast.291), kind=kOutput, calls=%fused_computation.191 | convolution fusion | flops 3523215360 | bytes 10305536 | tf_op jit(solution)/shard_map/dot_general | solution.py:60
  493.3 2.9 collective-permute-start.5
  496.1 93.0 %collective-permute-done.5 = bf16[280,1536]{1,0:T(8,128)(2,1)S(1)} collective-permute-done((bf16[280,1536]{1,0:T(8,128)(2,1)S(1)}, bf16[280,1536]{1,0:T(8,128)(2,1)S(1)}, u32[]{:S(2)}, u32[]{:S(2)}) %collective-permute-start.5) | collective-permute-done | bytes 860192 | tf_op jit(solution)/shard_map/ppermute | solution.py:229
  590.3 2.0 reshape.490
  593.5 3.6 all-to-all-start.7
  597.1 2.4 fusion.44
  601.0 14.5 %all-to-all-done.7 = bf16[8,280,192]{2,1,0:T(8,128)(2,1)S(1)} async-done(((bf16[8,280,192]{2,1,0:T(8,128)(2,1)}), bf16[8,280,192]{2,1,0:T(8,128)(2,1)S(1)}, u32[]{:S(2)}, u32[]{:S(2)}) %all-to-all-start.7) | async-done | bytes 860192 | tf_op jit(solution)/shard_map/all_to_all | solution.py:231
  615.5 4.3 all-to-all-start.6
  619.8 4.7 copy.190
  624.5 1.6 bitcast_convert_fusion
  626.1 2.9 copy.191
  629.0 13.4 %all-to-all-done.6 = bf16[8,1,384,280]{2,3,1,0:T(8,128)(2,1)} async-done(((bf16[8,1,384,280]{2,3,1,0:T(8,128)(2,1)}), bf16[8,1,384,280]{2,3,1,0:T(8,128)(2,1)}, u32[]{:S(2)}, u32[]{:S(2)}) %all-to-all-start.6) | async-done | bytes 1720352 | tf_op jit(solution)/shard_map/all_to_all | solution.py:217
  642.4 3.4 convert_element_type.389
  646.7 4.1 all-to-all-start.3
  650.9 3.1 convolution_multiply_fusion
  655.6 3.6 all-to-all-done.3
  660.6 3.9 fusion.76
  664.6 4.9 all-to-all-start.4
  674.3 9.8 %all-to-all-done.4 = bf16[4,384,192]{1,2,0:T(8,128)(2,1)S(1)} async-done(((bf16[4,384,192]{1,2,0:T(8,128)(2,1)}), bf16[4,384,192]{1,2,0:T(8,128)(2,1)S(1)}, u32[]{:S(2)}, u32[]{:S(2)}) %all-to-all-start.4) | async-done | bytes 589856 | tf_op jit(solution)/shard_map/all_to_all | solution.py:282
  684.1 3.5 all-to-all-start.1
  687.6 1.8 slice_bitcast_fusion.2
  690.3 7.0 all-to-all-done.1
  697.3 3.8 fusion.75
  701.0 4.2 all-to-all-start.2
  705.3 6.0 fusion.31
  711.6 39.9 %all-reduce = f32[32,160]{1,0:T(8,128)S(1)} all-reduce(f32[32,160]{1,0:T(8,128)S(1)} %pad_maximum_fusion.13), channel_id=6, replica_groups=mesh['ctx'=8,'fsdp'=4] {'ctx','fsdp'}, use_global_device_ids=true, to_apply=%region_15.16.clone | all-reduce | flops 5120 | bytes 40960
  752.6 3.1 fusion.50
  755.7 2.0 convert_reduce_fusion
  (235 shorter events, 57.4 us)
Async XLA Ops:
  7.2 76.1 %all-gather.10.cloned.1.call-start = ((), (), s32[]{:S(2)}) async-start(), calls=%async_computation.11 | async-start | bytes 6488064 | tf_op jit(solution)/shard_map/all_gather | solution.py:104
  9.3 101.2 %all-gather.12.cloned.1.call-start = ((), (), s32[]{:S(2)}) async-start(), calls=%async_computation.12 | async-start | bytes 1179648 | tf_op jit(solution)/shard_map/all_gather | solution.py:159
  25.0 58.3 %copy-start.34 = (f32[1536]{0:T(1024)}, f32[1536]{0:T(1024)S(1)}, u32[]{:S(2)}) copy-start(f32[1536]{0:T(1024)S(1)} %reshape.492) | copy-start | bytes 18436
  26.1 65.0 %copy-start.23 = (f32[128,128]{0,1:T(8,128)}, f32[128,128]{0,1:T(8,128)S(1)}, u32[]{:S(2)}) copy-start(f32[128,128]{0,1:T(8,128)S(1)} %get-tuple-element.54) | copy-start | bytes 196612
  26.1 64.9 %copy-start.25 = (f32[128,128]{0,1:T(8,128)}, f32[128,128]{0,1:T(8,128)S(1)}, u32[]{:S(2)}) copy-start(f32[128,128]{0,1:T(8,128)S(1)} %get-tuple-element.55) | copy-start | bytes 196612
  26.2 61.3 %copy-start.32 = (f32[128,128]{1,0:T(8,128)}, f32[128,128]{1,0:T(8,128)S(1)}, u32[]{:S(2)}) copy-start(f32[128,128]{1,0:T(8,128)S(1)} %copy.142) | copy-start | bytes 196612
  27.5 55.9 %copy-start.41 = (f32[128]{0:T(128)}, f32[128]{0:T(128)S(1)}, u32[]{:S(2)}) copy-start(f32[128]{0:T(128)S(1)} %add_rsqrt_fusion.1) | copy-start | bytes 1540
  28.6 58.5 %copy-start.6 = (bf16[128,1536]{1,0:T(8,128)(2,1)}, bf16[128,1536]{1,0:T(8,128)(2,1)S(1)}, u32[]{:S(2)}) copy-start(bf16[128,1536]{1,0:T(8,128)(2,1)S(1)} %fusion.25) | copy-start | bytes 1179652
  88.5 89.2 %all-gather.14.cloned.1.call-start = ((), (), s32[]{:S(2)}) async-start(), calls=%async_computation.13 | async-start | bytes 4866048 | tf_op jit(solution)/shard_map/all_gather | solution.py:110
  90.1 241.3 %all-gather.16.cloned.1.call-start = ((), (), s32[]{:S(2)}) async-start(), calls=%async_computation.14 | async-start | bytes 7077888 | tf_op jit(solution)/shard_map/all_gather | solution.py:69
  91.2 26.2 %copy-start.19 = (bf16[2,6,128,128]{2,3,1,0:T(8,128)(2,1)}, bf16[2,6,128,128]{2,3,1,0:T(8,128)(2,1)S(1)}, u32[]{:S(2)}) copy-start(bf16[2,6,128,128]{2,3,1,0:T(8,128)(2,1)S(1)} %fusion.49) | copy-start | bytes 1179652
  112.4 5.0 copy-start.11
  112.5 8.4 %copy-start.13 = (bf16[1024,2,128]{2,1,0:T(2,128)(2,1)}, bf16[1024,2,128]{2,1,0:T(2,128)(2,1)S(1)}, u32[]{:S(2)}) copy-start(bf16[1024,2,128]{2,1,0:T(2,128)(2,1)S(1)} %reshape.471) | copy-start | bytes 1572868
  120.9 56.8 %copy-start.4 = (bf16[1,128,1536]{2,1,0:T(8,128)(2,1)S(1)}, bf16[1,128,1536]{2,1,0:T(8,128)(2,1)}, u32[]{:S(2)}) copy-start(bf16[1,128,1536]{2,1,0:T(8,128)(2,1)} %param.11) | copy-start | bytes 1179652
  123.7 57.2 %copy-start.7 = (bf16[2,6,128,128]{2,3,1,0:T(8,128)(2,1)}, bf16[2,6,128,128]{2,3,1,0:T(8,128)(2,1)S(1)}, u32[]{:S(2)}) copy-start(bf16[2,6,128,128]{2,3,1,0:T(8,128)(2,1)S(1)} %get-tuple-element.60) | copy-start | bytes 1179652
  180.9 12.8 %copy-start.8 = (bf16[1,128,1536]{2,1,0:T(8,128)(2,1)S(1)}, bf16[1,128,1536]{2,1,0:T(8,128)(2,1)}, u32[]{:S(2)}) copy-start(bf16[1,128,1536]{2,1,0:T(8,128)(2,1)} %param.21) | copy-start | bytes 1179652
  180.9 11.5 %copy-start.36 = (f32[128]{0:T(128)}, f32[128]{0:T(128)S(1)}, u32[]{:S(2)}) copy-start(f32[128]{0:T(128)S(1)} %add_rsqrt_fusion) | copy-start | bytes 1540
  181.1 11.3 %collective-permute-start = (bf16[128,1536]{1,0:T(8,128)(2,1)S(1)}, bf16[128,1536]{1,0:T(8,128)(2,1)S(1)}, u32[]{:S(2)}, u32[]{:S(2)}) collective-permute-start(bf16[128,1536]{1,0:T(8,128)(2,1)S(1)} %multiply_convert_fusion.4), channel_id=1, source_target_pairs={{0,1},{1,0},{2,3},{3,2},{4,5},{5,4},{6,7},{7,6},{8,9},{9,8},{10,11... | collective-permute-start | bytes 1179656 | tf_op jit(solution)/shard_map/ppermute | solution.py:64
  193.4 153.0 %all-gather.18.cloned.1.call-start = ((), (), s32[]{:S(2)}) async-start(), calls=%async_computation.16 | async-start | bytes 7077888 | tf_op jit(solution)/shard_map/all_gather | solution.py:69
  193.7 10.5 %collective-permute-start.3 = (bf16[128,1536]{1,0:T(8,128)(2,1)S(1)}, bf16[128,1536]{1,0:T(8,128)(2,1)S(1)}, u32[]{:S(2)}, u32[]{:S(2)}) collective-permute-start(bf16[128,1536]{1,0:T(8,128)(2,1)S(1)} %bitcast.262), channel_id=1, source_target_pairs={{0,1},{1,0},{2,3},{3,2},{4,5},{5,4},{6,7},{7,6},{8,9},{9,8},{10,11... | collective-permute-start | bytes 1179656 | tf_op jit(solution)/shard_map/ppermute | solution.py:64
  217.3 4.6 copy-start.27
  218.3 3.6 copy-start.28
  224.6 100.2 %all-to-all-start = ((bf16[4,2,384,560]{2,3,1,0:T(8,128)(2,1)}), bf16[4,2,384,560]{2,3,1,0:T(8,128)(2,1)}, u32[]{:S(2)}, u32[]{:S(2)}) async-start(bf16[4,2,384,560]{2,3,1,0:T(8,128)(2,1)} %pad_maximum_fusion), calls=%async_computation | async-start | bytes 6881280 | tf_op jit(solution)/shard_map/all_to_all | solution.py:134
  229.3 201.5 %reduce-scatter.6.cloned.1.call-start = ((), (), s32[]{:S(2)}) async-start(), calls=%async_computation.17 | async-start | bytes 7077888 | tf_op jit(solution)/shard_map/reduce_scatter | solution.py:73
  230.6 115.8 %copy-start.30 = (bf16[280,1536]{1,0:T(8,128)(2,1)}, bf16[280,1536]{1,0:T(8,128)(2,1)S(1)}, u32[]{:S(2)}) copy-start(bf16[280,1536]{1,0:T(8,128)(2,1)S(1)} %constant_dynamic-slice_fusion.10) | copy-start | bytes 2580484
  230.6 115.8 %collective-permute-start.1 = (bf16[280,1536]{1,0:T(8,128)(2,1)S(1)}, bf16[280,1536]{1,0:T(8,128)(2,1)}, u32[]{:S(2)}, u32[]{:S(2)}) collective-permute-start(bf16[280,1536]{1,0:T(8,128)(2,1)S(1)} %constant_dynamic-slice_fusion.10), channel_id=1, source_target_pairs={{2,0},{3,1},{0,2},{1,3},{6,4},{7,5},{4,6},{5,7},{10,8},{11,9},{8,1... | collective-permute-start | bytes 2580488 | tf_op jit(solution)/shard_map/ppermute | solution.py:141
  331.4 9.2 %copy-start.5 = (bf16[2,1024,1536]{2,1,0:T(8,128)(2,1)S(1)}, bf16[2,1024,1536]{2,1,0:T(8,128)(2,1)}, u32[]{:S(2)}) copy-start(bf16[2,1024,1536]{2,1,0:T(8,128)(2,1)} %all-gather.16.cloned.1.call-done) | copy-start | bytes 18874372
  331.4 9.2 %copy-start.15 = (bf16[70,8,4,384]{3,1,2,0:T(8,128)(2,1)S(1)}, bf16[70,8,4,384]{3,1,2,0:T(8,128)(2,1)}, u32[]{:S(2)}) copy-start(bf16[70,8,4,384]{3,1,2,0:T(8,128)(2,1)} %copy.204) | copy-start | bytes 5160964
  346.4 10.8 %copy-start.16 = (bf16[70,8,4,384]{3,1,2,0:T(8,128)(2,1)S(1)}, bf16[70,8,4,384]{3,1,2,0:T(8,128)(2,1)}, u32[]{:S(2)}) copy-start(bf16[70,8,4,384]{3,1,2,0:T(8,128)(2,1)} %copy.204) | copy-start | bytes 5160964
  357.2 5.1 copy-start.46
  357.2 5.1 copy-start.47
  357.2 5.1 copy-start.14
  369.4 250.4 %all-gather.20.cloned.1.call-start = ((), (), s32[]{:S(2)}) async-start(), calls=%async_computation.19 | async-start | bytes 3538944 | tf_op jit(solution)/shard_map/all_gather | solution.py:272
  370.2 290.5 %all-gather.22.cloned.1.call-start = ((), (), s32[]{:S(2)}) async-start(), calls=%async_computation.20 | async-start | bytes 3538944 | tf_op jit(solution)/shard_map/all_gather | solution.py:272
  370.9 298.6 %reduce-scatter.8.cloned.1.call-start = ((), (), s32[]{:S(2)}) async-start(), calls=%async_computation.18 | async-start | bytes 1179648 | tf_op jit(solution)/shard_map/reduce_scatter | solution.py:255
  431.8 10.8 %collective-permute-start.4 = (bf16[128,1536]{1,0:T(8,128)(2,1)S(1)}, bf16[128,1536]{1,0:T(8,128)(2,1)S(1)}, u32[]{:S(2)}, u32[]{:S(2)}) collective-permute-start(bf16[128,1536]{1,0:T(8,128)(2,1)S(1)} %slice_bitcast_fusion), channel_id=1, source_target_pairs={{0,1},{1,0},{2,3},{3,2},{4,5},{5,4},{6,7},{7,6},{8,9},{9,8},{10,11... | collective-permute-start | bytes 1179656 | tf_op jit(solution)/shard_map/ppermute | solution.py:64
  433.4 9.2 %copy-start.10 = (bf16[2,128,1536]{2,1,0:T(8,128)(2,1)S(1)}, bf16[2,128,1536]{2,1,0:T(8,128)(2,1)}, u32[]{:S(2)}) copy-start(bf16[2,128,1536]{2,1,0:T(8,128)(2,1)} %reduce-scatter.6.cloned.1.call-done) | copy-start | bytes 2359300
  433.4 9.2 %copy-start.37 = (f32[128]{0:T(128)S(1)}, f32[128]{0:T(128)}, u32[]{:S(2)}) copy-start(f32[128]{0:T(128)} %copy-done.36) | copy-start | bytes 1540
  442.6 5.4 copy-start.9
  442.9 5.0 copy-start.43
  443.2 6.1 copy-start.40
  449.3 5.6 copy-start.20
  461.3 7.5 copy-start.17
  471.3 5.0 copy-start.31
  471.3 122.2 %all-to-all-start.5 = ((bf16[4,2,384,560]{2,3,1,0:T(8,128)(2,1)}), bf16[4,2,384,560]{2,3,1,0:T(8,128)(2,1)}, u32[]{:S(2)}, u32[]{:S(2)}) async-start(bf16[4,2,384,560]{2,3,1,0:T(8,128)(2,1)} %copy.169), calls=%async_computation.8 | async-start | bytes 6881280 | tf_op jit(solution)/shard_map/all_to_all | solution.py:202
  476.2 211.4 %reduce-scatter.4.cloned.1.call-start = ((), (), s32[]{:S(2)}) async-start(), calls=%async_computation.15 | async-start | bytes 7077888 | tf_op jit(solution)/shard_map/reduce_scatter | solution.py:73
  493.3 95.9 %collective-permute-start.5 = (bf16[280,1536]{1,0:T(8,128)(2,1)S(1)}, bf16[280,1536]{1,0:T(8,128)(2,1)S(1)}, u32[]{:S(2)}, u32[]{:S(2)}) collective-permute-start(bf16[280,1536]{1,0:T(8,128)(2,1)S(1)} %slice.196), channel_id=1, source_target_pairs={{0,2},{1,3},{2,0},{3,1},{4,6},{5,7},{6,4},{7,5},{8,10},{9,11},{10,... | collective-permute-start | bytes 2580488 | tf_op jit(solution)/shard_map/ppermute | solution.py:229
  593.5 21.9 %all-to-all-start.7 = ((bf16[8,280,192]{2,1,0:T(8,128)(2,1)}), bf16[8,280,192]{2,1,0:T(8,128)(2,1)S(1)}, u32[]{:S(2)}, u32[]{:S(2)}) async-start(bf16[8,280,192]{2,1,0:T(8,128)(2,1)} %bitcast.245), calls=%async_computation.10 | async-start | bytes 2293760 | tf_op jit(solution)/shard_map/all_to_all | solution.py:231
  615.5 26.9 %all-to-all-start.6 = ((bf16[8,1,384,280]{2,3,1,0:T(8,128)(2,1)}), bf16[8,1,384,280]{2,3,1,0:T(8,128)(2,1)}, u32[]{:S(2)}, u32[]{:S(2)}) async-start(bf16[8,1,384,280]{2,3,1,0:T(8,128)(2,1)} %bitcast.249), calls=%async_computation.9 | async-start | bytes 3440640 | tf_op jit(solution)/shard_map/all_to_all | solution.py:217
  629.0 21.8 %copy-start.12 = (bf16[1024,2,128,1]{0,2,3,1:T(8,128)(2,1)S(1)}, bf16[1024,2,128,1]{0,2,3,1:T(8,128)(2,1)}, u32[]{:S(2)}) copy-start(bf16[1024,2,128,1]{0,2,3,1:T(8,128)(2,1)} %copy-done.11) | copy-start | bytes 1572868
  645.8 8.1 %copy-start.26 = (f32[128,128]{0,1:T(8,128)S(1)}, f32[128,128]{0,1:T(8,128)}, u32[]{:S(2)}) copy-start(f32[128,128]{0,1:T(8,128)} %copy-done.25) | copy-start | bytes 196612
  646.7 12.4 %all-to-all-start.3 = ((bf16[8,128,192]{1,2,0:T(8,128)(2,1)}), bf16[8,128,192]{1,2,0:T(8,128)(2,1)}, u32[]{:S(2)}, u32[]{:S(2)}) async-start(bf16[8,128,192]{1,2,0:T(8,128)(2,1)} %bitcast.68), calls=%async_computation.6 | async-start | bytes 786432 | tf_op jit(solution)/shard_map/all_to_all | solution.py:274
  660.6 10.8 %copy-start.33 = (f32[128,128]{1,0:T(8,128)S(1)}, f32[128,128]{1,0:T(8,128)}, u32[]{:S(2)}) copy-start(f32[128,128]{1,0:T(8,128)} %copy-done.32) | copy-start | bytes 196612
  664.6 7.3 copy-start.22
  664.6 8.5 %copy-start.18 = (bf16[128,1536]{0,1:T(8,128)(2,1)S(1)}, bf16[128,1536]{0,1:T(8,128)(2,1)}, u32[]{:S(2)}) copy-start(bf16[128,1536]{0,1:T(8,128)(2,1)} %fusion.35) | copy-start | bytes 1179652
  664.6 19.6 %all-to-all-start.4 = ((bf16[4,384,192]{1,2,0:T(8,128)(2,1)}), bf16[4,384,192]{1,2,0:T(8,128)(2,1)S(1)}, u32[]{:S(2)}, u32[]{:S(2)}) async-start(bf16[4,384,192]{1,2,0:T(8,128)(2,1)} %fusion.76), calls=%async_computation.7 | async-start | bytes 1179648 | tf_op jit(solution)/shard_map/all_to_all | solution.py:282
  684.1 13.1 %all-to-all-start.1 = ((bf16[8,128,256]{2,1,0:T(8,128)(2,1)}), bf16[8,128,256]{2,1,0:T(8,128)(2,1)S(1)}, u32[]{:S(2)}, u32[]{:S(2)}) async-start(bf16[8,128,256]{2,1,0:T(8,128)(2,1)} %bitcast.60), calls=%async_computation.4 | async-start | bytes 1048576 | tf_op jit(solution)/shard_map/all_to_all | solution.py:274
  689.4 63.2 %collective-permute-start.2 = (bf16[128,1536]{1,0:T(8,128)(2,1)}, bf16[128,1536]{1,0:T(8,128)(2,1)}, u32[]{:S(2)}, u32[]{:S(2)}) collective-permute-start(bf16[128,1536]{1,0:T(8,128)(2,1)} %slice_bitcast_fusion.2), channel_id=1, source_target_pairs={{0,1},{1,0},{2,3},{3,2},{4,5},{5,4},{6,7},{7,6},{8,9},{9,8},{10,11... | collective-permute-start | bytes 1179656 | tf_op jit(solution)/shard_map/ppermute | solution.py:64
  697.3 8.0 %copy-start.35 = (f32[1536]{0:T(1024)S(1)}, f32[1536]{0:T(1024)}, u32[]{:S(2)}) copy-start(f32[1536]{0:T(1024)} %copy-done.34) | copy-start | bytes 18436
  697.3 8.0 %copy-start.42 = (f32[128]{0:T(128)S(1)}, f32[128]{0:T(128)}, u32[]{:S(2)}) copy-start(f32[128]{0:T(128)} %copy-done.41) | copy-start | bytes 1540
  701.0 54.7 %all-to-all-start.2 = ((bf16[4,384,256]{2,1,0:T(8,128)(2,1)}), bf16[4,384,256]{2,1,0:T(8,128)(2,1)}, u32[]{:S(2)}, u32[]{:S(2)}) async-start(bf16[4,384,256]{2,1,0:T(8,128)(2,1)} %fusion.75), calls=%async_computation.5 | async-start | bytes 1572864 | tf_op jit(solution)/shard_map/all_to_all | solution.py:282
  705.3 47.3 %copy-start.38 = (f32[128]{0:T(128)S(1)}, f32[128]{0:T(128)}, u32[]{:S(2)}) copy-start(f32[128]{0:T(128)} %copy-done.36) | copy-start | bytes 1540
  705.3 47.3 %copy-start.44 = (f32[128]{0:T(128)S(1)}, f32[128]{0:T(128)}, u32[]{:S(2)}) copy-start(f32[128]{0:T(128)} %copy-done.43) | copy-start | bytes 1540
  705.3 52.4 %copy-start.1 = (bf16[384,2048]{1,0:T(8,128)(2,1)S(1)}, bf16[384,2048]{1,0:T(8,128)(2,1)}, u32[]{:S(2)}) copy-start(bf16[384,2048]{1,0:T(8,128)(2,1)} %param.15) | copy-start | bytes 4718596
  (8 other events, 17.9 us)
Sparse Core Ops, SparseCore 0:
  11.4 71.8 all-gather.9
  88.6 21.8 all-gather.11
  114.0 63.6 all-gather.13
  193.5 43.6 all-gather.15
  239.0 45.3 all-gather.17
  369.5 61.2 reduce-scatter.5
  432.7 32.1 all-gather.19
  466.8 32.7 all-gather.21
  502.7 35.9 reduce-scatter.7
  541.9 63.7 reduce-scatter.3
where the time goes:
time: 774 us; the launch traced here: 765 us
  waiting for transfers between devices  432 us (56%)
  matrix products  113 us (15%)
  local copies, waits for them, and re-layouts  66.2 us (9%)
  blocking collectives  54.8 us (7%)
  starting transfers between devices  45.1 us (6%)
  other arithmetic  37.7 us (5%)
  between operations  15.7 us (2%)
    dot_general x15, matrix products, dot(): lax.dot_general(left, right, (dims, ((), ())), preferred_element_type=out)  96.1 us
    ppermute x1, waiting for transfers between devices, body(): lax.ppermute(grad_down[b], 'fsdp', route).astype(F32)  93 us
    all_to_all x1, waiting for transfers between devices, body(): got = lax.all_to_all(sent, 'fsdp', split_axis=0, concat_axis=0, tiled=True)  91.3 us
    all_gather x1, waiting for transfers between devices, body(): lax.all_gather(lax.dynamic_slice_in_dim(projection, place * slab, slab, 0...  54.7 us
    all_gather x1, waiting for transfers between devices, body(): lax.all_gather(lax.dynamic_slice_in_dim(output_weight, place * slab, slab...  53.9 us
    reduce_scatter x2, waiting for transfers between devices, scatter_tokens(): parts = lax.psum_scatter(partial, 'ctx', scatter_dimension=1, tiled=True)  50.9 us
    unnamed x1, blocking collectives  39.9 us
    ppermute x4, waiting for transfers between devices, swapped(): return lax.ppermute(x, 'fsdp', [(i, i ^ 1) for i in range(size)])  19.5 us
  transfers between devices with their start and end apart: 24, of which 14 were waited for; matrix products, arithmetic and copies ran while one was open for 23% of the time, Pallas kernels for 0%

commit v1 on v0

--- a/solution.py
+++ b/solution.py
@@ -14,6 +14,19 @@
 NEGATIVE = -1e30
 BF = jnp.bfloat16
 F32 = jnp.float32
+
+
+def collect(value, axis, dim):
+    ways = lax.axis_size(axis)
+    up = [(d, (d + 1) % ways) for d in range(ways)]
+    down = [(d, (d - 1) % ways) for d in range(ways)]
+    earlier, later = ([value], [value])
+    for _ in range(ways // 2):
+        earlier.append(lax.ppermute(earlier[-1], axis, up))
+    for _ in range((ways - 1) // 2):
+        later.append(lax.ppermute(later[-1], axis, down))
+    line = jnp.concatenate([*earlier[::-1], *later[1:]], axis=dim)
+    return jnp.roll(line, (lax.axis_index(axis) - ways // 2) * value.shape[dim], axis=dim)
 
 
 def rope_tables(places):
@@ -156,9 +169,7 @@
         sine,
     ).astype(BF)
     values = projected[:, query_width + key_width :].astype(BF)
-    pairs = lax.all_gather(
-        jnp.concatenate([keys.reshape(rows, key_width), values], axis=1), "ctx", axis=0, tiled=True
-    )
+    pairs = collect(jnp.concatenate([keys.reshape(rows, key_width), values], axis=1), "ctx", 0)
     all_keys = pairs[:, :key_width].reshape(length, KV_HEADS, HEAD)
     all_values = pairs[:, key_width:].reshape(length, KV_HEADS, HEAD)
     grouped = queries.reshape(rows, KV_HEADS, ratio, HEAD).transpose(1, 2, 0, 3)

time: 774 us -> 742 us (0.959)
  waiting for transfers between devices: 432 us -> 394 us
  starting transfers between devices: 45.1 us -> 53.2 us
    all_gather x1, waiting for transfers between devices: 53.9 us -> 19.4 us  [body(): lax.all_gather(lax.dynamic_slice_in_dim(output_weight, place * slab, slab...]
    all_gather x1 -> x0, waiting for transfers between devices: 19.4 us -> none  [body(): lax.all_gather(jnp.concatenate([keys.reshape(rows, key_width), values], a...]
    ppermute x0 -> x7, waiting for transfers between devices: none -> 15.4 us  [the longest x4 15 us: collect(): earlier.append(lax.ppermute(earlier[-1], axis, up))]
    ppermute x0 -> x7, starting transfers between devices: none -> 8.28 us  [the longest x3 8.02 us: collect(): later.append(lax.ppermute(later[-1], axis, down))]
    unnamed x109 -> x106, local copies, waits for them, and re-layouts: 18.2 us -> 18.4 us
  transfers between devices with their start and end apart: 24 -> 30, of which waited for: 14 -> 18; matrix products, arithmetic and copies ran while one was open for 23% -> 25% of each run, Pallas kernels for 0% -> 0%
where the time goes in v1:
time: 742 us; the launch traced here: 733 us
  waiting for transfers between devices  394 us (53%)
  matrix products  110 us (15%)
  local copies, waits for them, and re-layouts  64.3 us (9%)
  blocking collectives  54.8 us (7%)
  starting transfers between devices  53.2 us (7%)
  other arithmetic  40.6 us (5%)
  between operations  15.5 us (2%)
    ppermute x1, waiting for transfers between devices, body(): lax.ppermute(grad_down[b], 'fsdp', route).astype(F32)  93.6 us
    dot_general x15, matrix products, dot(): lax.dot_general(left, right, (dims, ((), ())), preferred_element_type=out)  93.4 us
    all_to_all x1, waiting for transfers between devices, body(): got = lax.all_to_all(sent, 'fsdp', split_axis=0, concat_axis=0, tiled=True)  91.2 us
    all_gather x1, waiting for transfers between devices, body(): lax.all_gather(lax.dynamic_slice_in_dim(projection, place * slab, slab, 0...  51.3 us
    reduce_scatter x2, waiting for transfers between devices, scatter_tokens(): parts = lax.psum_scatter(partial, 'ctx', scatter_dimension=1, tiled=True)  51.1 us
    unnamed x1, blocking collectives  39.9 us
    all_gather x1, waiting for transfers between devices, body(): lax.all_gather(lax.dynamic_slice_in_dim(output_weight, place * slab, slab...  19.4 us
    ppermute x4, waiting for transfers between devices, swapped(): return lax.ppermute(x, 'fsdp', [(i, i ^ 1) for i in range(size)])  19.4 us
  transfers between devices with their start and end apart: 30, of which 18 were waited for; matrix products, arithmetic and copies ran while one was open for 25% of the time, Pallas kernels for 0%

profile of v1, /device:TPU:0, one launch (start us, length us, event | category | flops | bytes accessed | tf_op | source)
XLA Modules:
  0.0 733.0 jit_solution(14396253699496193858)
XLA Ops:
  11.8 15.0 %all-gather.1 = bf16[4,1,1280]{2,1,0:T(2,128)(2,1)S(1)} all-gather(bf16[1,1,1280]{2,1,0:T(2,128)(2,1)S(1)} %reshape.500), channel_id=2, replica_groups=mesh['ctx'=8,'fsdp'=4] {'fsdp'}, dimensions={0}, use_global_device_ids=true | all-gather | bytes 12800 | tf_op jit(solution)/shard_map/all_gather | solution.py:129
  31.9 51.3 %all-gather.9.cloned.1.call-done = bf16[1536,2048]{1,0:T(8,128)(2,1)} async-done(((bf16[48,2048]{1,0:T(8,128)(2,1)}), bf16[1536,2048]{1,0:T(8,128)(2,1)}) %all-gather.9.cloned.1.call-update) | async-done | bytes 6291472 | tf_op jit(solution)/shard_map/all_gather | solution.py:117
  83.3 3.8 convolution_add_fusion.1
  88.7 5.2 collective-permute-done
  94.7 2.6 collective-permute-start.4
  97.7 3.5 collective-permute-done.1
  101.3 2.7 collective-permute-start.5
  104.0 3.5 collective-permute-done.2
  107.7 2.7 collective-permute-start.6
  110.3 2.7 collective-permute-done.3
  118.2 4.8 fusion.70
  123.1 3.5 fusion.5
  128.2 2.1 fusion.71
  130.3 19.4 %all-gather.11.cloned.1.call-done = bf16[1536,1536]{1,0:T(8,128)(2,1)} async-done(((bf16[48,1536]{1,0:T(8,128)(2,1)}), bf16[1536,1536]{1,0:T(8,128)(2,1)}) %all-gather.11.cloned.1.call-update) | async-done | bytes 4718608 | tf_op jit(solution)/shard_map/all_gather | solution.py:123
  149.8 3.2 multiply_reduce_fusion.3
  154.8 9.7 %collective-permute-done.7 = bf16[128,1536]{1,0:T(8,128)(2,1)S(1)} collective-permute-done((bf16[128,1536]{1,0:T(8,128)(2,1)S(1)}, bf16[128,1536]{1,0:T(8,128)(2,1)S(1)}, u32[]{:S(2)}, u32[]{:S(2)}) %collective-permute-start.7) | collective-permute-done | bytes 393248 | tf_op jit(solution)/shard_map/ppermute | solution.py:77
  167.2 9.0 %collective-permute-done.10 = bf16[128,1536]{1,0:T(8,128)(2,1)S(1)} collective-permute-done((bf16[128,1536]{1,0:T(8,128)(2,1)S(1)}, bf16[128,1536]{1,0:T(8,128)(2,1)S(1)}, u32[]{:S(2)}, u32[]{:S(2)}) %collective-permute-start.10) | collective-permute-done | bytes 393248 | tf_op jit(solution)/shard_map/ppermute | solution.py:77
  177.2 4.1 constant_dynamic-slice_fusion.6
  190.8 2.0 pad_maximum_fusion
  192.8 4.7 all-to-all-start
  198.8 2.9 collective-permute-start.8
  201.7 91.2 %all-to-all-done = bf16[4,2,384,560]{2,3,1,0:T(8,128)(2,1)} async-done(((bf16[4,2,384,560]{2,3,1,0:T(8,128)(2,1)}), bf16[4,2,384,560]{2,3,1,0:T(8,128)(2,1)}, u32[]{:S(2)}, u32[]{:S(2)}) %all-to-all-start) | async-done | bytes 3440672 | tf_op jit(solution)/shard_map/all_to_all | solution.py:147
  292.8 2.3 fusion.68
  299.5 9.2 %fusion.73 = f32[2048,560]{0,1:T(8,128)} fusion(bf16[2048,1536]{1,0:T(8,128)(2,1)} %bitcast.254, bf16[1536,560]{0,1:T(8,128)(2,1)} %bitcast.276), kind=kOutput, calls=%fused_computation.204 | convolution fusion | flops 3523215360 | bytes 12599296 | tf_op jit(solution)/shard_map/dot_general | solution.py:73
  308.7 5.8 fusion.72
  314.5 10.8 %multiply_convert_fusion.1 = (bf16[2048,560]{0,1:T(8,128)(2,1)S(1)}, bf16[2048,560]{0,1:T(8,128)(2,1)S(1)}, bf16[2048,560]{0,1:T(8,128)(2,1)}) fusion(f32[2048,560]{0,1:T(8,128)} %fusion.72, f32[2048,560]{0,1:T(8,128)} %fusion.73, bf16[2048,1536]{1,0:T(8,128)(2,1)} %bitcast.292, bf16[280,1536]{1,0:T(8,128)(2,1)} %collective-permute-done.8, ...), kind=kOutput, calls=%fused_computation.6 | convolution fusion | flops 3545006080 | bytes 24068096 | tf_op jit(solution)/shard_map/dot_general | solution.py:73
  325.3 5.1 fusion.74
  330.4 7.0 add_convert_fusion
  338.9 9.1 %copy.168 = bf16[1536,2048]{1,0:T(8,128)(2,1)} copy(bf16[1536,2048]{0,1:T(8,128)(2,1)} %bitcast.255) | data formatting | bytes 12582912 | tf_op jit(solution)/shard_map/dot_general | solution.py:73
  348.0 51.1 %reduce-scatter.6.cloned.1.call-done = bf16[2,128,1536]{2,1,0:T(8,128)(2,1)} async-done(((bf16[2,1024,1536]{2,1,0:T(8,128)(2,1)}), bf16[2,128,1536]{2,1,0:T(8,128)(2,1)}) %reduce-scatter.6.cloned.1.call-update) | async-done | bytes 786448 | tf_op jit(solution)/shard_map/reduce_scatter | solution.py:86
  401.7 8.6 %fusion.10 = bf16[4,1,384,560]{2,3,0,1:T(8,128)(2,1)} fusion(bf16[4,384,2048]{2,1,0:T(8,128)(2,1)} %bitcast.258, bf16[2048,560]{0,1:T(8,128)(2,1)} %copy-done.36), kind=kOutput, calls=%fused_computation.28 | convolution fusion | flops 3523215360 | bytes 10305536 | tf_op jit(solution)/shard_map/dot_general | solution.py:73
  411.5 2.4 convolution_convert_fusion
  416.4 3.9 multiply_convert_fusion
  422.7 2.5 fusion.18
  426.5 7.4 %fusion.13 = bf16[4,1,384,560]{2,3,0,1:T(8,128)(2,1)S(1)} fusion(bf16[4,384,2048]{2,1,0:T(8,128)(2,1)} %bitcast.259, bf16[2048,560]{0,1:T(8,128)(2,1)} %copy-done.37), kind=kOutput, calls=%fused_computation.29 | convolution fusion | flops 3523215360 | bytes 10305536 | tf_op jit(solution)/shard_map/dot_general | solution.py:73
  434.3 2.1 copy.169
  436.5 4.8 all-to-all-start.5
  441.3 9.3 %fusion.24 = bf16[2048,1536]{1,0:T(8,128)(2,1)} fusion(bf16[2048,560]{0,1:T(8,128)(2,1)} %get-tuple-element.25, bf16[280,1536]{1,0:T(8,128)(2,1)} %collective-permute-done.8, bf16[280,1536]{1,0:T(8,128)(2,1)S(1)} %copy-done.28), kind=kOutput, calls=%fused_computation.46 | convolution fusion | flops 3526656000 | bytes 10305536 | tf_op jit(solution)/shard_map/dot_general | solution.py:73
  450.6 7.2 fusion.77
  457.9 2.9 collective-permute-start.12
  460.8 93.6 %collective-permute-done.12 = bf16[280,1536]{1,0:T(8,128)(2,1)S(1)} collective-permute-done((bf16[280,1536]{1,0:T(8,128)(2,1)S(1)}, bf16[280,1536]{1,0:T(8,128)(2,1)S(1)}, u32[]{:S(2)}, u32[]{:S(2)}) %collective-permute-start.12) | collective-permute-done | bytes 860192 | tf_op jit(solution)/shard_map/ppermute | solution.py:240
  555.5 2.0 reshape.490
  558.7 3.6 all-to-all-start.7
  562.3 2.3 fusion.44
  566.1 17.7 %all-to-all-done.7 = bf16[8,280,192]{2,1,0:T(8,128)(2,1)S(1)} async-done(((bf16[8,280,192]{2,1,0:T(8,128)(2,1)}), bf16[8,280,192]{2,1,0:T(8,128)(2,1)S(1)}, u32[]{:S(2)}, u32[]{:S(2)}) %all-to-all-start.7) | async-done | bytes 860192 | tf_op jit(solution)/shard_map/all_to_all | solution.py:242
  583.7 4.3 all-to-all-start.6
  588.1 4.7 copy.190
  594.4 2.9 copy.191
  597.3 13.4 %all-to-all-done.6 = bf16[8,1,384,280]{2,3,1,0:T(8,128)(2,1)} async-done(((bf16[8,1,384,280]{2,3,1,0:T(8,128)(2,1)}), bf16[8,1,384,280]{2,3,1,0:T(8,128)(2,1)}, u32[]{:S(2)}, u32[]{:S(2)}) %all-to-all-start.6) | async-done | bytes 1720352 | tf_op jit(solution)/shard_map/all_to_all | solution.py:228
  610.6 3.4 convert_element_type.389
  615.0 4.1 all-to-all-start.3
  619.1 3.1 convolution_multiply_fusion
  623.9 3.6 all-to-all-done.3
  628.9 3.9 fusion.76
  632.8 5.0 all-to-all-start.4
  642.6 9.8 %all-to-all-done.4 = bf16[4,384,192]{1,2,0:T(8,128)(2,1)S(1)} async-done(((bf16[4,384,192]{1,2,0:T(8,128)(2,1)}), bf16[4,384,192]{1,2,0:T(8,128)(2,1)S(1)}, u32[]{:S(2)}, u32[]{:S(2)}) %all-to-all-start.4) | async-done | bytes 589856 | tf_op jit(solution)/shard_map/all_to_all | solution.py:293
  652.4 3.5 all-to-all-start.1
  658.6 7.0 all-to-all-done.1
  665.6 3.8 fusion.75
  669.4 4.2 all-to-all-start.2
  673.6 6.0 fusion.31
  679.9 39.9 %all-reduce = f32[32,160]{1,0:T(8,128)S(1)} all-reduce(f32[32,160]{1,0:T(8,128)S(1)} %pad_maximum_fusion.13), channel_id=6, replica_groups=mesh['ctx'=8,'fsdp'=4] {'ctx','fsdp'}, use_global_device_ids=true, to_apply=%region_15.16.clone | all-reduce | flops 5120 | bytes 40960
  720.9 3.1 fusion.50
  724.0 2.0 convert_reduce_fusion
  (247 shorter events, 69.6 us)
Async XLA Ops:
  7.2 76.1 %all-gather.9.cloned.1.call-start = ((), (), s32[]{:S(2)}) async-start(), calls=%async_computation.11 | async-start | bytes 6488064 | tf_op jit(solution)/shard_map/all_gather | solution.py:117
  9.3 140.5 %all-gather.11.cloned.1.call-start = ((), (), s32[]{:S(2)}) async-start(), calls=%async_computation.12 | async-start | bytes 4866048 | tf_op jit(solution)/shard_map/all_gather | solution.py:123
  11.0 288.5 %all-gather.13.cloned.1.call-start = ((), (), s32[]{:S(2)}) async-start(), calls=%async_computation.13 | async-start | bytes 7077888 | tf_op jit(solution)/shard_map/all_gather | solution.py:82
  26.8 60.3 %copy-start.32 = (f32[1536]{0:T(1024)}, f32[1536]{0:T(1024)S(1)}, u32[]{:S(2)}) copy-start(f32[1536]{0:T(1024)S(1)} %reshape.492) | copy-start | bytes 18436
  27.8 79.7 %copy-start.23 = (f32[128,128]{0,1:T(8,128)}, f32[128,128]{0,1:T(8,128)S(1)}, u32[]{:S(2)}) copy-start(f32[128,128]{0,1:T(8,128)S(1)} %get-tuple-element.54) | copy-start | bytes 196612
  27.8 79.7 %copy-start.25 = (f32[128,128]{0,1:T(8,128)}, f32[128,128]{0,1:T(8,128)S(1)}, u32[]{:S(2)}) copy-start(f32[128,128]{0,1:T(8,128)S(1)} %get-tuple-element.55) | copy-start | bytes 196612
  27.9 59.5 %copy-start.29 = (f32[128,128]{1,0:T(8,128)}, f32[128,128]{1,0:T(8,128)S(1)}, u32[]{:S(2)}) copy-start(f32[128,128]{1,0:T(8,128)S(1)} %copy.142) | copy-start | bytes 196612
  30.7 56.3 %copy-start.34 = (f32[128]{0:T(128)}, f32[128]{0:T(128)S(1)}, u32[]{:S(2)}) copy-start(f32[128]{0:T(128)S(1)} %add_rsqrt_fusion.1) | copy-start | bytes 1540
  31.9 55.2 %copy-start.6 = (bf16[128,1536]{1,0:T(8,128)(2,1)}, bf16[128,1536]{1,0:T(8,128)(2,1)S(1)}, u32[]{:S(2)}) copy-start(bf16[128,1536]{1,0:T(8,128)(2,1)S(1)} %fusion.25) | copy-start | bytes 1179652
  87.7 19.9 %copy-start.21 = (f32[128,2,128]{2,1,0:T(2,128)}, f32[128,2,128]{2,1,0:T(2,128)S(1)}, u32[]{:S(2)}) copy-start(f32[128,2,128]{2,1,0:T(2,128)S(1)} %mul.308) | copy-start | bytes 393220
  88.4 5.5 collective-permute-start
  93.9 7.3 collective-permute-start.1
  94.7 6.6 collective-permute-start.4
  101.2 6.3 collective-permute-start.2
  101.3 6.4 collective-permute-start.5
  107.5 5.6 collective-permute-start.3
  107.6 10.5 %copy-start.19 = (bf16[2,6,128,128]{2,3,1,0:T(8,128)(2,1)}, bf16[2,6,128,128]{2,3,1,0:T(8,128)(2,1)S(1)}, u32[]{:S(2)}) copy-start(bf16[2,6,128,128]{2,3,1,0:T(8,128)(2,1)S(1)} %fusion.49) | copy-start | bytes 1179652
  107.7 7.7 %collective-permute-start.6 = (bf16[128,512]{1,0:T(8,128)(2,1)S(1)}, bf16[128,512]{1,0:T(8,128)(2,1)S(1)}, u32[]{:S(2)}, u32[]{:S(2)}) collective-permute-start(bf16[128,512]{1,0:T(8,128)(2,1)S(1)} %collective-permute-done.5), channel_id=1, source_target_pairs={{0,28},{4,0},{8,4},{12,8},{16,12},{20,16},{24,20},{28,24},{1,29},{... | collective-permute-start | bytes 393224 | tf_op jit(solution)/shard_map/ppermute | solution.py:27
  118.0 5.0 copy-start.11
  118.2 8.4 %copy-start.13 = (bf16[1024,2,128]{2,1,0:T(2,128)(2,1)}, bf16[1024,2,128]{2,1,0:T(2,128)(2,1)S(1)}, u32[]{:S(2)}) copy-start(bf16[1024,2,128]{2,1,0:T(2,128)(2,1)S(1)} %reshape.471) | copy-start | bytes 1572868
  126.6 23.2 %copy-start.4 = (bf16[1,128,1536]{2,1,0:T(8,128)(2,1)S(1)}, bf16[1,128,1536]{2,1,0:T(8,128)(2,1)}, u32[]{:S(2)}) copy-start(bf16[1,128,1536]{2,1,0:T(8,128)(2,1)} %param.11) | copy-start | bytes 1179652
  130.3 22.7 %copy-start.7 = (bf16[2,6,128,128]{2,3,1,0:T(8,128)(2,1)}, bf16[2,6,128,128]{2,3,1,0:T(8,128)(2,1)S(1)}, u32[]{:S(2)}) copy-start(bf16[2,6,128,128]{2,3,1,0:T(8,128)(2,1)S(1)} %get-tuple-element.60) | copy-start | bytes 1179652
  153.0 12.7 %copy-start.8 = (bf16[1,128,1536]{2,1,0:T(8,128)(2,1)S(1)}, bf16[1,128,1536]{2,1,0:T(8,128)(2,1)}, u32[]{:S(2)}) copy-start(bf16[1,128,1536]{2,1,0:T(8,128)(2,1)} %param.21) | copy-start | bytes 1179652
  153.2 11.3 %collective-permute-start.7 = (bf16[128,1536]{1,0:T(8,128)(2,1)S(1)}, bf16[128,1536]{1,0:T(8,128)(2,1)S(1)}, u32[]{:S(2)}, u32[]{:S(2)}) collective-permute-start(bf16[128,1536]{1,0:T(8,128)(2,1)S(1)} %multiply_convert_fusion.4), channel_id=1, source_target_pairs={{0,1},{1,0},{2,3},{3,2},{4,5},{5,4},{6,7},{7,6},{8,9},{9,8},{10,11... | collective-permute-start | bytes 1179656 | tf_op jit(solution)/shard_map/ppermute | solution.py:77
  165.5 149.0 %all-gather.15.cloned.1.call-start = ((), (), s32[]{:S(2)}) async-start(), calls=%async_computation.15 | async-start | bytes 7077888 | tf_op jit(solution)/shard_map/all_gather | solution.py:82
  165.7 10.5 %collective-permute-start.10 = (bf16[128,1536]{1,0:T(8,128)(2,1)S(1)}, bf16[128,1536]{1,0:T(8,128)(2,1)S(1)}, u32[]{:S(2)}, u32[]{:S(2)}) collective-permute-start(bf16[128,1536]{1,0:T(8,128)(2,1)S(1)} %bitcast.264), channel_id=1, source_target_pairs={{0,1},{1,0},{2,3},{3,2},{4,5},{5,4},{6,7},{7,6},{8,9},{9,8},{10,11... | collective-permute-start | bytes 1179656 | tf_op jit(solution)/shard_map/ppermute | solution.py:77
  192.8 100.0 %all-to-all-start = ((bf16[4,2,384,560]{2,3,1,0:T(8,128)(2,1)}), bf16[4,2,384,560]{2,3,1,0:T(8,128)(2,1)}, u32[]{:S(2)}, u32[]{:S(2)}) async-start(bf16[4,2,384,560]{2,3,1,0:T(8,128)(2,1)} %pad_maximum_fusion), calls=%async_computation | async-start | bytes 6881280 | tf_op jit(solution)/shard_map/all_to_all | solution.py:147
  197.5 201.5 %reduce-scatter.6.cloned.1.call-start = ((), (), s32[]{:S(2)}) async-start(), calls=%async_computation.16 | async-start | bytes 7077888 | tf_op jit(solution)/shard_map/reduce_scatter | solution.py:86
  198.8 115.6 %copy-start.27 = (bf16[280,1536]{1,0:T(8,128)(2,1)}, bf16[280,1536]{1,0:T(8,128)(2,1)S(1)}, u32[]{:S(2)}) copy-start(bf16[280,1536]{1,0:T(8,128)(2,1)S(1)} %constant_dynamic-slice_fusion.10) | copy-start | bytes 2580484
  198.8 115.6 %collective-permute-start.8 = (bf16[280,1536]{1,0:T(8,128)(2,1)S(1)}, bf16[280,1536]{1,0:T(8,128)(2,1)}, u32[]{:S(2)}, u32[]{:S(2)}) collective-permute-start(bf16[280,1536]{1,0:T(8,128)(2,1)S(1)} %constant_dynamic-slice_fusion.10), channel_id=1, source_target_pairs={{2,0},{3,1},{0,2},{1,3},{6,4},{7,5},{4,6},{5,7},{10,8},{11,9},{8,1... | collective-permute-start | bytes 2580488 | tf_op jit(solution)/shard_map/ppermute | solution.py:154
  299.4 9.2 %copy-start.5 = (bf16[2,1024,1536]{2,1,0:T(8,128)(2,1)S(1)}, bf16[2,1024,1536]{2,1,0:T(8,128)(2,1)}, u32[]{:S(2)}) copy-start(bf16[2,1024,1536]{2,1,0:T(8,128)(2,1)} %all-gather.13.cloned.1.call-done) | copy-start | bytes 18874372
  299.4 9.2 %copy-start.15 = (bf16[70,8,4,384]{3,1,2,0:T(8,128)(2,1)S(1)}, bf16[70,8,4,384]{3,1,2,0:T(8,128)(2,1)}, u32[]{:S(2)}) copy-start(bf16[70,8,4,384]{3,1,2,0:T(8,128)(2,1)} %copy.204) | copy-start | bytes 5160964
  314.5 10.8 %copy-start.16 = (bf16[70,8,4,384]{3,1,2,0:T(8,128)(2,1)S(1)}, bf16[70,8,4,384]{3,1,2,0:T(8,128)(2,1)}, u32[]{:S(2)}) copy-start(bf16[70,8,4,384]{3,1,2,0:T(8,128)(2,1)} %copy.204) | copy-start | bytes 5160964
  325.2 5.1 copy-start.36
  325.2 5.1 copy-start.37
  325.3 5.1 copy-start.14
  337.5 250.6 %all-gather.17.cloned.1.call-start = ((), (), s32[]{:S(2)}) async-start(), calls=%async_computation.18 | async-start | bytes 3538944 | tf_op jit(solution)/shard_map/all_gather | solution.py:283
  338.1 290.8 %all-gather.19.cloned.1.call-start = ((), (), s32[]{:S(2)}) async-start(), calls=%async_computation.19 | async-start | bytes 3538944 | tf_op jit(solution)/shard_map/all_gather | solution.py:283
  338.8 299.0 %reduce-scatter.8.cloned.1.call-start = ((), (), s32[]{:S(2)}) async-start(), calls=%async_computation.17 | async-start | bytes 1179648 | tf_op jit(solution)/shard_map/reduce_scatter | solution.py:266
  338.9 72.6 %slice-start = ((s8[4718592]{0:T(1024)(128)(4,1)}), s8[524288]{0:T(1024)(128)(4,1)S(1)}, s32[]{:S(2)}) async-start(s8[4718592]{0:T(1024)(128)(4,1)} %bitcast.247), calls=%async_computation.20 | async-start | bytes 1048576
  400.1 10.8 %collective-permute-start.11 = (bf16[128,1536]{1,0:T(8,128)(2,1)S(1)}, bf16[128,1536]{1,0:T(8,128)(2,1)S(1)}, u32[]{:S(2)}, u32[]{:S(2)}) collective-permute-start(bf16[128,1536]{1,0:T(8,128)(2,1)S(1)} %slice_bitcast_fusion), channel_id=1, source_target_pairs={{0,1},{1,0},{2,3},{3,2},{4,5},{5,4},{6,7},{7,6},{8,9},{9,8},{10,11... | collective-permute-start | bytes 1179656 | tf_op jit(solution)/shard_map/ppermute | solution.py:77
  401.6 9.2 %copy-start.10 = (bf16[2,128,1536]{2,1,0:T(8,128)(2,1)S(1)}, bf16[2,128,1536]{2,1,0:T(8,128)(2,1)}, u32[]{:S(2)}) copy-start(bf16[2,128,1536]{2,1,0:T(8,128)(2,1)} %reduce-scatter.6.cloned.1.call-done) | copy-start | bytes 2359300
  401.6 9.9 %slice-start.1 = ((s8[4718592]{0:T(1024)(128)(4,1)}), s8[4194304]{0:T(1024)(128)(4,1)S(1)}, s32[]{:S(2)}) async-start(s8[4718592]{0:T(1024)(128)(4,1)} %bitcast.247), calls=%async_computation.21 | async-start | bytes 8388608
  416.4 5.6 copy-start.20
  426.5 7.4 %copy-start.17 = (bf16[4,1,384,560]{2,3,0,1:T(8,128)(2,1)S(1)}, bf16[4,1,384,560]{2,3,0,1:T(8,128)(2,1)}, u32[]{:S(2)}) copy-start(bf16[4,1,384,560]{2,3,0,1:T(8,128)(2,1)} %fusion.10) | copy-start | bytes 5160964
  436.5 4.9 copy-start.28
  436.5 122.2 %all-to-all-start.5 = ((bf16[4,2,384,560]{2,3,1,0:T(8,128)(2,1)}), bf16[4,2,384,560]{2,3,1,0:T(8,128)(2,1)}, u32[]{:S(2)}, u32[]{:S(2)}) async-start(bf16[4,2,384,560]{2,3,1,0:T(8,128)(2,1)} %copy.169), calls=%async_computation.8 | async-start | bytes 6881280 | tf_op jit(solution)/shard_map/all_to_all | solution.py:213
  441.3 214.7 %reduce-scatter.4.cloned.1.call-start = ((), (), s32[]{:S(2)}) async-start(), calls=%async_computation.14 | async-start | bytes 7077888 | tf_op jit(solution)/shard_map/reduce_scatter | solution.py:86
  457.9 96.4 %collective-permute-start.12 = (bf16[280,1536]{1,0:T(8,128)(2,1)S(1)}, bf16[280,1536]{1,0:T(8,128)(2,1)S(1)}, u32[]{:S(2)}, u32[]{:S(2)}) collective-permute-start(bf16[280,1536]{1,0:T(8,128)(2,1)S(1)} %slice.194), channel_id=1, source_target_pairs={{0,2},{1,3},{2,0},{3,1},{4,6},{5,7},{6,4},{7,5},{8,10},{9,11},{10,... | collective-permute-start | bytes 2580488 | tf_op jit(solution)/shard_map/ppermute | solution.py:240
  558.7 25.1 %all-to-all-start.7 = ((bf16[8,280,192]{2,1,0:T(8,128)(2,1)}), bf16[8,280,192]{2,1,0:T(8,128)(2,1)S(1)}, u32[]{:S(2)}, u32[]{:S(2)}) async-start(bf16[8,280,192]{2,1,0:T(8,128)(2,1)} %bitcast.245), calls=%async_computation.10 | async-start | bytes 2293760 | tf_op jit(solution)/shard_map/all_to_all | solution.py:242
  583.7 26.9 %all-to-all-start.6 = ((bf16[8,1,384,280]{2,3,1,0:T(8,128)(2,1)}), bf16[8,1,384,280]{2,3,1,0:T(8,128)(2,1)}, u32[]{:S(2)}, u32[]{:S(2)}) async-start(bf16[8,1,384,280]{2,3,1,0:T(8,128)(2,1)} %bitcast.251), calls=%async_computation.9 | async-start | bytes 3440640 | tf_op jit(solution)/shard_map/all_to_all | solution.py:228
  597.3 21.8 %copy-start.12 = (bf16[1024,2,128,1]{0,2,3,1:T(8,128)(2,1)S(1)}, bf16[1024,2,128,1]{0,2,3,1:T(8,128)(2,1)}, u32[]{:S(2)}) copy-start(bf16[1024,2,128,1]{0,2,3,1:T(8,128)(2,1)} %copy-done.11) | copy-start | bytes 1572868
  614.1 8.1 %copy-start.26 = (f32[128,128]{0,1:T(8,128)S(1)}, f32[128,128]{0,1:T(8,128)}, u32[]{:S(2)}) copy-start(f32[128,128]{0,1:T(8,128)} %copy-done.25) | copy-start | bytes 196612
  615.0 12.4 %all-to-all-start.3 = ((bf16[8,128,192]{1,2,0:T(8,128)(2,1)}), bf16[8,128,192]{1,2,0:T(8,128)(2,1)}, u32[]{:S(2)}, u32[]{:S(2)}) async-start(bf16[8,128,192]{1,2,0:T(8,128)(2,1)} %bitcast.68), calls=%async_computation.6 | async-start | bytes 786432 | tf_op jit(solution)/shard_map/all_to_all | solution.py:285
  628.9 10.8 %copy-start.30 = (f32[128,128]{1,0:T(8,128)S(1)}, f32[128,128]{1,0:T(8,128)}, u32[]{:S(2)}) copy-start(f32[128,128]{1,0:T(8,128)} %copy-done.29) | copy-start | bytes 196612
  632.8 7.4 %copy-start.22 = (f32[128,2,128]{2,1,0:T(2,128)S(1)}, f32[128,2,128]{2,1,0:T(2,128)}, u32[]{:S(2)}) copy-start(f32[128,2,128]{2,1,0:T(2,128)} %copy-done.21) | copy-start | bytes 393220
  632.8 8.5 %copy-start.18 = (bf16[128,1536]{0,1:T(8,128)(2,1)S(1)}, bf16[128,1536]{0,1:T(8,128)(2,1)}, u32[]{:S(2)}) copy-start(bf16[128,1536]{0,1:T(8,128)(2,1)} %fusion.35) | copy-start | bytes 1179652
  632.8 19.6 %all-to-all-start.4 = ((bf16[4,384,192]{1,2,0:T(8,128)(2,1)}), bf16[4,384,192]{1,2,0:T(8,128)(2,1)S(1)}, u32[]{:S(2)}, u32[]{:S(2)}) async-start(bf16[4,384,192]{1,2,0:T(8,128)(2,1)} %fusion.76), calls=%async_computation.7 | async-start | bytes 1179648 | tf_op jit(solution)/shard_map/all_to_all | solution.py:293
  652.4 13.1 %all-to-all-start.1 = ((bf16[8,128,256]{2,1,0:T(8,128)(2,1)}), bf16[8,128,256]{2,1,0:T(8,128)(2,1)S(1)}, u32[]{:S(2)}, u32[]{:S(2)}) async-start(bf16[8,128,256]{2,1,0:T(8,128)(2,1)} %bitcast.60), calls=%async_computation.4 | async-start | bytes 1048576 | tf_op jit(solution)/shard_map/all_to_all | solution.py:285
  657.7 63.2 %collective-permute-start.9 = (bf16[128,1536]{1,0:T(8,128)(2,1)}, bf16[128,1536]{1,0:T(8,128)(2,1)}, u32[]{:S(2)}, u32[]{:S(2)}) collective-permute-start(bf16[128,1536]{1,0:T(8,128)(2,1)} %slice_bitcast_fusion.2), channel_id=1, source_target_pairs={{0,1},{1,0},{2,3},{3,2},{4,5},{5,4},{6,7},{7,6},{8,9},{9,8},{10,11... | collective-permute-start | bytes 1179656 | tf_op jit(solution)/shard_map/ppermute | solution.py:77
  665.6 8.0 %copy-start.33 = (f32[1536]{0:T(1024)S(1)}, f32[1536]{0:T(1024)}, u32[]{:S(2)}) copy-start(f32[1536]{0:T(1024)} %copy-done.32) | copy-start | bytes 18436
  665.6 8.0 %copy-start.35 = (f32[128]{0:T(128)S(1)}, f32[128]{0:T(128)}, u32[]{:S(2)}) copy-start(f32[128]{0:T(128)} %copy-done.34) | copy-start | bytes 1540
  669.4 54.6 %all-to-all-start.2 = ((bf16[4,384,256]{2,1,0:T(8,128)(2,1)}), bf16[4,384,256]{2,1,0:T(8,128)(2,1)}, u32[]{:S(2)}, u32[]{:S(2)}) async-start(bf16[4,384,256]{2,1,0:T(8,128)(2,1)} %fusion.75), calls=%async_computation.5 | async-start | bytes 1572864 | tf_op jit(solution)/shard_map/all_to_all | solution.py:293
  673.6 52.4 %copy-start.1 = (bf16[384,2048]{1,0:T(8,128)(2,1)S(1)}, bf16[384,2048]{1,0:T(8,128)(2,1)}, u32[]{:S(2)}) copy-start(bf16[384,2048]{1,0:T(8,128)(2,1)} %param.15) | copy-start | bytes 4718596
  (6 other events, 10.4 us)
Sparse Core Ops, SparseCore 0:
  11.4 71.7 all-gather.8
  86.7 62.9 all-gather.10
  165.6 43.6 all-gather.12
  211.1 45.3 all-gather.14
  337.6 61.4 reduce-scatter.5
  400.8 32.1 all-gather.16
  434.9 32.7 all-gather.18
  470.9 35.9 reduce-scatter.7
  510.3 69.9 reduce-scatter.3
